TPU v7x, 32 devices: a whole 2x2x4 slice. The times are simulated.
32 devices in a mesh: section: 2 (over x), expert: 4 (over z), tensor: 4 (over y, core).
Axes of the slice: x: 2, y: 2, z: 4, core: 2. Of those that a mesh axis runs over, the one named last changes fastest.
Arguments:
- layer_inputs: bfloat16 [2, 2, 320, 3072], P('section', None, 'expert', 'tensor'), may hold values from -6 to 6
- grad_out: bfloat16 [2, 320, 3072], P(None, 'expert', 'tensor'), may hold values from -6 to 6
- norm_gain: bfloat16 [2, 3072], P('section', 'tensor'), may hold values from 0.25 to 1.75
- router_w: bfloat16 [2, 3072, 4], P('section', 'tensor'), may hold values from -0.21875 to 0.21875
- w_gate: bfloat16 [2, 3072, 32768], P('section', None, ('expert', 'tensor')), may hold values from -0.109375 to 0.109375
- w_up: bfloat16 [2, 3072, 32768], P('section', None, ('expert', 'tensor')), may hold values from -0.109375 to 0.109375
- w_down: bfloat16 [2, 32768, 3072], P('section', ('expert', 'tensor')), may hold values from -0.0625 to 0.0625
- saved_gate: bfloat16 [2, 2, 4, 64, 32768], P('section', None, None, None, ('expert', 'tensor')), may hold values from -6 to 6
- saved_up: bfloat16 [2, 2, 4, 64, 32768], P('section', None, None, None, ('expert', 'tensor')), may hold values from -6 to 6
- routes: int32 [2, 2, 320, 2], P('section', None, 'expert'), may hold values from 0 to 3, all different within a row; in each aligned block of 80 rows (0 to 79, 80 to 159, ..., all dimensions but the last counted through in order) at most 64 rows name the same one
Outputs:
- layer_grads: bfloat16 [2, 2, 320, 3072], P('section', None, 'expert', 'tensor')
Inputs may be any that keep to these rules, and one draw needn't show every extreme that they name: `routes`: each token names two different experts; within the 80 tokens of one device's aligned block of a layer and micro-batch, no expert is named by more than 64 tokens, and in some blocks one expert is named by exactly 64.
All inputs are finite; a program needn't handle non-finite values.
Results may differ from a plain program's by a relative error of at most 0.011.
Values may be sent and summed in bfloat16 or wider, within the bound.
A program may use at most 128 MiB of HBM per device.

v0:
```python
import jax
import jax.numpy as jnp
from jax import lax
from jax.sharding import PartitionSpec as P

norm_eps = 1e-05
highest = lax.Precision.HIGHEST


def from_behind(block, axis, distance):
    devices = range(lax.axis_size(axis))
    route = [(i - distance, i) for i in devices if i - distance in devices]
    return lax.ppermute(block, axis, route)


def on_device(
    layer_inputs, grad_out, norm_gain, router_w, w_gate, w_up, w_down, saved_gate, saved_up, routes
):
    sections = lax.axis_size("section")
    position = lax.axis_index("section")
    holders = lax.axis_size("expert")
    micros = grad_out.shape[0]
    tokens_here = grad_out.shape[1]
    quarter = grad_out.shape[2]
    gain_full = norm_gain[0].astype(jnp.float32)
    router = router_w[0]
    gate_mat = w_gate[0]
    up_mat = w_up[0]
    down_mat = w_down[0]
    width_all = gate_mat.shape[0]
    experts = router.shape[1]
    group = holders // experts
    capacity = saved_gate.shape[3]
    slot_count = experts * capacity
    slot_ids = jnp.arange(slot_count, dtype=jnp.int32)
    expert_ids = jnp.arange(experts, dtype=jnp.int32)

    def add_columns(piece):
        return jnp.einsum("scw,fw->scf", piece, down_mat, preferred_element_type=jnp.float32)

    def layer_back(inputs, upstream, chosen, gate_saved, up_saved):
        values = inputs.astype(jnp.float32)
        squares = lax.psum(jnp.sum(values * values, axis=-1), "tensor")
        scale = lax.rsqrt(squares / width_all + norm_eps)[:, None]
        normed = (values * scale * gain_full).astype(jnp.bfloat16)
        partial_logits = jnp.dot(normed, router, preferred_element_type=jnp.float32)
        logits = lax.psum(partial_logits, "tensor")
        onehot = (chosen[:, :, None] == expert_ids[None, None, :]).astype(jnp.float32)
        picked = jnp.sum(onehot * logits[:, None, :], axis=-1)
        first = jax.nn.sigmoid(picked[:, 0] - picked[:, 1])
        second = jax.nn.sigmoid(picked[:, 1] - picked[:, 0])
        flat_hot = onehot.reshape(tokens_here * 2, experts)
        earlier = jnp.cumsum(flat_hot, axis=0) - flat_hot
        within = jnp.sum(earlier * flat_hot, axis=-1).astype(jnp.int32)
        target = chosen.reshape(tokens_here * 2) * capacity + within
        placing = (
            (slot_ids[:, None] == target[None, :])
            .astype(jnp.float32)
            .reshape(slot_count, tokens_here, 2)
        )
        select = jnp.sum(placing, axis=-1).astype(jnp.bfloat16)
        upstream_send = jnp.dot(select, upstream, preferred_element_type=jnp.float32).astype(
            jnp.bfloat16
        )
        copies = jnp.broadcast_to(
            upstream_send.reshape(experts, 1, capacity, quarter),
            (experts, group, capacity, quarter),
        ).reshape(holders, capacity, quarter)
        arrived = lax.all_to_all(copies, "expert", split_axis=0, concat_axis=0, tiled=True)
        back_act = add_columns(lax.all_gather(arrived, "tensor", axis=2, tiled=True))
        gate_act = gate_saved.astype(jnp.float32)
        up_act = up_saved.astype(jnp.float32)
        sigma = jax.nn.sigmoid(gate_act)
        swish = gate_act * sigma
        weight_part = jnp.sum(swish * up_act * back_act, axis=-1)
        slope = sigma * (1.0 + gate_act * (1.0 - sigma))
        gate_grad = (back_act * up_act * slope).astype(jnp.bfloat16)
        up_grad = (back_act * swish).astype(jnp.bfloat16)
        unit = jnp.einsum("scf,df->scd", gate_grad, gate_mat, preferred_element_type=jnp.float32)
        unit = unit + jnp.einsum("scf,df->scd", up_grad, up_mat, preferred_element_type=jnp.float32)
        weighted = placing[:, :, 0] * first[None, :] + placing[:, :, 1] * second[None, :]
        unit_share = lax.psum_scatter(unit, "tensor", scatter_dimension=2, tiled=True)
        back_units, back_weights = (
            lax.all_to_all(unit_share, "expert", split_axis=0, concat_axis=0, tiled=True),
            lax.all_to_all(weight_part, "expert", split_axis=0, concat_axis=0, tiled=True),
        )
        slot_units = jnp.sum(back_units.reshape(experts, group, capacity, quarter), axis=1).reshape(
            slot_count, quarter
        )
        slot_weight = jnp.sum(back_weights.reshape(experts, group, capacity), axis=1).reshape(
            slot_count
        )
        hidden_grad = lax.dot_general(
            weighted, slot_units, (((0,), (0,)), ((), ())), precision=highest
        )
        prob_part = jnp.einsum("stk,s->tk", placing, slot_weight, precision=highest)
        prob_grad = lax.psum(prob_part, "tensor")
        logit_step = first * second * (prob_grad[:, 0] - prob_grad[:, 1])
        logit_grad = (onehot[:, 0, :] - onehot[:, 1, :]) * logit_step[:, None]
        hidden_grad = hidden_grad + jnp.einsum(
            "te,de->td", logit_grad, router.astype(jnp.float32), precision=highest
        )
        gained = hidden_grad * gain_full
        moment = lax.psum(jnp.sum(values * gained, axis=-1), "tensor")[:, None] / width_all
        result = (
            upstream.astype(jnp.float32) + scale * gained - values * scale * scale * scale * moment
        )
        return result.astype(jnp.bfloat16)

    def advance(tick, carry):
        incoming, grads = carry
        micro_id = tick - (sections - 1 - position)
        valid = jnp.logical_and(micro_id >= 0, micro_id < micros)
        safe_id = jnp.clip(micro_id, 0, micros - 1)
        inputs = lax.dynamic_index_in_dim(layer_inputs[0], safe_id, 0, keepdims=False)
        top_grad = lax.dynamic_index_in_dim(grad_out, safe_id, 0, keepdims=False)
        chosen = lax.dynamic_index_in_dim(routes[0], safe_id, 0, keepdims=False)
        gate_saved = lax.dynamic_index_in_dim(saved_gate[0], safe_id, 0, keepdims=False)
        up_saved = lax.dynamic_index_in_dim(saved_up[0], safe_id, 0, keepdims=False)
        upstream = jnp.where(position == sections - 1, top_grad, incoming)
        computed = layer_back(inputs, upstream, chosen, gate_saved, up_saved)
        result = jnp.where(valid, computed, jnp.zeros_like(computed))
        updated = lax.dynamic_update_index_in_dim(grads, result, safe_id, 0)
        grads = jnp.where(valid, updated, grads)
        incoming = from_behind(result, "section", -1)
        return (incoming, grads)

    start = (
        jnp.zeros((tokens_here, quarter), jnp.bfloat16),
        jnp.zeros((micros, tokens_here, quarter), jnp.bfloat16),
    )
    final_in, grads = lax.fori_loop(0, micros + sections - 1, advance, start)
    return grads[None]


def solution(mesh):
    placed = (
        P("section", None, "expert", "tensor"),
        P(None, "expert", "tensor"),
        P("section", "tensor"),
        P("section", "tensor", None),
        P("section", None, ("expert", "tensor")),
        P("section", None, ("expert", "tensor")),
        P("section", ("expert", "tensor"), None),
        P("section", None, None, None, ("expert", "tensor")),
        P("section", None, None, None, ("expert", "tensor")),
        P("section", None, "expert", None),
    )
    return jax.shard_map(
        on_device,
        mesh=mesh,
        in_specs=placed,
        out_specs=P("section", None, "expert", "tensor"),
        check_vma=False,
    )
```

profile of v0, /device:TPU:0, one launch (start us, length us, event | category | flops | bytes accessed | tf_op | source)
XLA Modules:
  0.0 453.6 jit_solution(15014488951981677367)
XLA Ops:
  7.3 438.8 %while.19 = (s32[]{:T(128)}, bf16[80,768]{1,0:T(8,128)(2,1)S(1)}, bf16[2,80,768]{2,1,0:T(8,128)(2,1)S(1)}, s32[]{:T(128)}, pred[]{:T(512)}, /*index=5*/bf16[2,80...) while((s32[]{:T(128)}, bf16[80,768]{1,0:T(8,128)(2,1)S(1)}, ...), condition=%wide.region_14.15_spmd.clone.clone, body=%wide.region_0.14_spmd.clone.clone.sunk | while | flops 9905498112 | bytes 112821912 | solution.py:132
  12.3 17.9 %all_to_all.47 = bf16[4,64,768]{2,1,0:T(8,128)(2,1)} all-to-all(bf16[4,64,768]{2,1,0:T(8,128)(2,1)S(1)} %bitcast.166), channel_id=1, replica_groups=mesh['section'=2,'expert'=4,'tensor'=4] {'expert'}, dimensions={0} | all-to-all | bytes 786432 | tf_op jit(solution)/shard_map/while/body/eval_jaxpr/all_to_all | solution.py:69
  30.3 18.8 %all-gather.2.cloned.1.call-done = bf16[4,64,3072]{2,1,0:T(8,128)(2,1)} async-done(((bf16[4,64,768]{2,1,0:T(8,128)(2,1)}), bf16[4,64,3072]{2,1,0:T(8,128)(2,1)}) %all-gather.2.cloned.1.call-update) | async-done | bytes 1572880 | tf_op jit(solution)/shard_map/while/body/eval_jaxpr/all_gather | solution.py:70
  49.2 9.9 %fusion.123 = (f32[4,64]{1,0:T(4,128)}, f32[4,64,2048]{2,1,0:T(8,128)S(1)}) fusion(bf16[1,2,4,64,2048]{4,3,2,1,0:T(8,128)(2,1)S(1)} %copy-done.5, s32[]{:T(128)S(6)} %min.13, bf16[1,2,4,64,2048]{4,3,2,1,0:T(8,128)(2,1)} %get-tuple-element.699, bf16[4,64,3072]{2,1,0:T(8,128)(2,1)} %all-gather.2.cloned.1.call-done, ...), kind=kOutput, calls=%fused_computation.17.clone.1 | convolution fusion | flops 3225943808 | bytes 18351108 | tf_op jit(solution)/shard_map/while/body/eval_jaxpr/scw,fw->scf/dot_general | solution.py:39
  59.1 10.7 %fusion.129 = f32[4,64,3072]{2,1,0:T(8,128)} fusion(bf16[3072,2048]{1,0:T(8,128)(2,1)} %get-tuple-element.701, f32[4,64,2048]{2,1,0:T(8,128)S(1)} %get-tuple-element.640, bf16[1,2,4,64,2048]{4,3,2,1,0:T(8,128)(2,1)S(1)} %copy-done.6, s32[]{:T(128)S(6)} %min.13), kind=kOutput, calls=%fused_computation.2.clone.1 | convolution fusion | flops 3224895488 | bytes 18874372 | tf_op jit(solution)/shard_map/while/body/eval_jaxpr/scf,df->scd/dot_general | solution.py:80
  69.8 11.6 %fusion.130 = f32[4,64,3072]{2,1,0:T(8,128)} fusion(f32[4,64,3072]{2,1,0:T(8,128)} %fusion.129, bf16[3072,2048]{1,0:T(8,128)(2,1)} %get-tuple-element.700, f32[4,64,2048]{2,1,0:T(8,128)} %copy-done.7, bf16[1,2,4,64,2048]{4,3,2,1,0:T(8,128)(2,1)S(1)} %copy-done.6, s32[]{:T(128)S(6)} %min.13, bf16[1,2,4,64,2048]{4,3,2,1,0:T(8,128)(2,1)S(1)} %copy-done.5), kind=kOutput, calls=%fused_computation.8.clone.1 | convolution fusion | flops 3228303360 | bytes 23068676 | tf_op jit(solution)/shard_map/while/body/eval_jaxpr/scf,df->scd/dot_general | solution.py:79
  82.5 5.9 %psum.62 = f32[80]{0:T(128)S(1)} all-reduce(f32[80]{0:T(128)S(1)} %fusion.125), channel_id=1, replica_groups=mesh['section'=2,'expert'=4,'tensor'=4] {'tensor'}, use_global_device_ids=true, to_apply=%region_2.2 | all-reduce | flops 80 | bytes 640 | tf_op jit(solution)/shard_map/while/body/eval_jaxpr/psum | solution.py:43
  93.3 5.5 %all-to-all-done.1 = f32[4,1,64]{2,1,0:T(1,128)S(1)} async-done(((f32[4,1,64]{2,1,0:T(1,128)}), f32[4,1,64]{2,1,0:T(1,128)S(1)}, u32[]{:S(2)}, u32[]{:S(2)}) %all-to-all-start.1) | async-done | bytes 1056 | tf_op jit(solution)/shard_map/while/body/eval_jaxpr/all_to_all | solution.py:85
  98.8 20.5 %reduce-scatter.2.cloned.1.call-done = f32[4,64,768]{2,1,0:T(8,128)} async-done(((f32[4,64,3072]{2,1,0:T(8,128)}), f32[4,64,768]{2,1,0:T(8,128)}) %reduce-scatter.2.cloned.1.call-update) | async-done | bytes 786448 | tf_op jit(solution)/shard_map/while/body/eval_jaxpr/reduce_scatter | solution.py:82
  125.5 6.1 %all-reduce.3 = (f32[80,2]{0,1:T(2,128)S(1)}, f32[80,4]{0,1:T(4,128)S(1)}) all-reduce(f32[80,2]{0,1:T(2,128)S(1)} %bitcast.172, f32[80,4]{0,1:T(4,128)S(1)} %fusion.126), channel_id=1, replica_groups=mesh['section'=2,'expert'=4,'tensor'=4] {'tensor'}, use_global_device_ids=true, to_apply=%region_11.11 | all-reduce | flops 480 | bytes 3840 | tf_op jit(solution)/shard_map/while/body/eval_jaxpr/psum | solution.py:97
  131.9 12.0 %all-to-all-done.2 = f32[4,64,768]{2,1,0:T(8,128)S(1)} async-done(((f32[4,64,768]{2,1,0:T(8,128)}), f32[4,64,768]{2,1,0:T(8,128)S(1)}, u32[]{:S(2)}, u32[]{:S(2)}) %all-to-all-start.2) | async-done | bytes 786464 | tf_op jit(solution)/shard_map/while/body/eval_jaxpr/all_to_all | solution.py:84
  144.6 5.9 %psum.63 = f32[80]{0:T(128)S(1)} all-reduce(f32[80]{0:T(128)S(1)} %get-tuple-element.643), channel_id=1, replica_groups=mesh['section'=2,'expert'=4,'tensor'=4] {'tensor'}, use_global_device_ids=true, to_apply=%region_13.13 | all-reduce | flops 80 | bytes 640 | tf_op jit(solution)/shard_map/while/body/eval_jaxpr/psum | solution.py:104
  162.5 13.6 %all_to_all.47 = bf16[4,64,768]{2,1,0:T(8,128)(2,1)} all-to-all(bf16[4,64,768]{2,1,0:T(8,128)(2,1)S(1)} %bitcast.166), channel_id=1, replica_groups=mesh['section'=2,'expert'=4,'tensor'=4] {'expert'}, dimensions={0} | all-to-all | bytes 786432 | tf_op jit(solution)/shard_map/while/body/eval_jaxpr/all_to_all | solution.py:69
  176.2 17.3 %all-gather.2.cloned.1.call-done = bf16[4,64,3072]{2,1,0:T(8,128)(2,1)} async-done(((bf16[4,64,768]{2,1,0:T(8,128)(2,1)}), bf16[4,64,3072]{2,1,0:T(8,128)(2,1)}) %all-gather.2.cloned.1.call-update) | async-done | bytes 1572880 | tf_op jit(solution)/shard_map/while/body/eval_jaxpr/all_gather | solution.py:70
  193.5 9.9 %fusion.123 = (f32[4,64]{1,0:T(4,128)}, f32[4,64,2048]{2,1,0:T(8,128)S(1)}) fusion(bf16[1,2,4,64,2048]{4,3,2,1,0:T(8,128)(2,1)S(1)} %copy-done.5, s32[]{:T(128)S(6)} %min.13, bf16[1,2,4,64,2048]{4,3,2,1,0:T(8,128)(2,1)} %get-tuple-element.699, bf16[4,64,3072]{2,1,0:T(8,128)(2,1)} %all-gather.2.cloned.1.call-done, ...), kind=kOutput, calls=%fused_computation.17.clone.1 | convolution fusion | flops 3225943808 | bytes 18351108 | tf_op jit(solution)/shard_map/while/body/eval_jaxpr/scw,fw->scf/dot_general | solution.py:39
  203.3 10.7 %fusion.129 = f32[4,64,3072]{2,1,0:T(8,128)} fusion(bf16[3072,2048]{1,0:T(8,128)(2,1)} %get-tuple-element.701, f32[4,64,2048]{2,1,0:T(8,128)S(1)} %get-tuple-element.640, bf16[1,2,4,64,2048]{4,3,2,1,0:T(8,128)(2,1)S(1)} %copy-done.6, s32[]{:T(128)S(6)} %min.13), kind=kOutput, calls=%fused_computation.2.clone.1 | convolution fusion | flops 3224895488 | bytes 18874372 | tf_op jit(solution)/shard_map/while/body/eval_jaxpr/scf,df->scd/dot_general | solution.py:80
  214.0 11.6 %fusion.130 = f32[4,64,3072]{2,1,0:T(8,128)} fusion(f32[4,64,3072]{2,1,0:T(8,128)} %fusion.129, bf16[3072,2048]{1,0:T(8,128)(2,1)} %get-tuple-element.700, f32[4,64,2048]{2,1,0:T(8,128)} %copy-done.7, bf16[1,2,4,64,2048]{4,3,2,1,0:T(8,128)(2,1)S(1)} %copy-done.6, s32[]{:T(128)S(6)} %min.13, bf16[1,2,4,64,2048]{4,3,2,1,0:T(8,128)(2,1)S(1)} %copy-done.5), kind=kOutput, calls=%fused_computation.8.clone.1 | convolution fusion | flops 3228303360 | bytes 23068676 | tf_op jit(solution)/shard_map/while/body/eval_jaxpr/scf,df->scd/dot_general | solution.py:79
  226.8 5.9 %psum.62 = f32[80]{0:T(128)S(1)} all-reduce(f32[80]{0:T(128)S(1)} %fusion.125), channel_id=1, replica_groups=mesh['section'=2,'expert'=4,'tensor'=4] {'tensor'}, use_global_device_ids=true, to_apply=%region_2.2 | all-reduce | flops 80 | bytes 640 | tf_op jit(solution)/shard_map/while/body/eval_jaxpr/psum | solution.py:43
  243.1 20.5 %reduce-scatter.2.cloned.1.call-done = f32[4,64,768]{2,1,0:T(8,128)} async-done(((f32[4,64,3072]{2,1,0:T(8,128)}), f32[4,64,768]{2,1,0:T(8,128)}) %reduce-scatter.2.cloned.1.call-update) | async-done | bytes 786448 | tf_op jit(solution)/shard_map/while/body/eval_jaxpr/reduce_scatter | solution.py:82
  269.8 6.1 %all-reduce.3 = (f32[80,2]{0,1:T(2,128)S(1)}, f32[80,4]{0,1:T(4,128)S(1)}) all-reduce(f32[80,2]{0,1:T(2,128)S(1)} %bitcast.172, f32[80,4]{0,1:T(4,128)S(1)} %fusion.126), channel_id=1, replica_groups=mesh['section'=2,'expert'=4,'tensor'=4] {'tensor'}, use_global_device_ids=true, to_apply=%region_11.11 | all-reduce | flops 480 | bytes 3840 | tf_op jit(solution)/shard_map/while/body/eval_jaxpr/psum | solution.py:97
  276.2 11.9 %all-to-all-done.2 = f32[4,64,768]{2,1,0:T(8,128)S(1)} async-done(((f32[4,64,768]{2,1,0:T(8,128)}), f32[4,64,768]{2,1,0:T(8,128)S(1)}, u32[]{:S(2)}, u32[]{:S(2)}) %all-to-all-start.2) | async-done | bytes 786464 | tf_op jit(solution)/shard_map/while/body/eval_jaxpr/all_to_all | solution.py:84
  288.9 5.9 %psum.63 = f32[80]{0:T(128)S(1)} all-reduce(f32[80]{0:T(128)S(1)} %get-tuple-element.643), channel_id=1, replica_groups=mesh['section'=2,'expert'=4,'tensor'=4] {'tensor'}, use_global_device_ids=true, to_apply=%region_13.13 | all-reduce | flops 80 | bytes 640 | tf_op jit(solution)/shard_map/while/body/eval_jaxpr/psum | solution.py:104
  306.8 13.6 %all_to_all.47 = bf16[4,64,768]{2,1,0:T(8,128)(2,1)} all-to-all(bf16[4,64,768]{2,1,0:T(8,128)(2,1)S(1)} %bitcast.166), channel_id=1, replica_groups=mesh['section'=2,'expert'=4,'tensor'=4] {'expert'}, dimensions={0} | all-to-all | bytes 786432 | tf_op jit(solution)/shard_map/while/body/eval_jaxpr/all_to_all | solution.py:69
  320.5 17.3 %all-gather.2.cloned.1.call-done = bf16[4,64,3072]{2,1,0:T(8,128)(2,1)} async-done(((bf16[4,64,768]{2,1,0:T(8,128)(2,1)}), bf16[4,64,3072]{2,1,0:T(8,128)(2,1)}) %all-gather.2.cloned.1.call-update) | async-done | bytes 1572880 | tf_op jit(solution)/shard_map/while/body/eval_jaxpr/all_gather | solution.py:70
  337.8 9.9 %fusion.123 = (f32[4,64]{1,0:T(4,128)}, f32[4,64,2048]{2,1,0:T(8,128)S(1)}) fusion(bf16[1,2,4,64,2048]{4,3,2,1,0:T(8,128)(2,1)S(1)} %copy-done.5, s32[]{:T(128)S(6)} %min.13, bf16[1,2,4,64,2048]{4,3,2,1,0:T(8,128)(2,1)} %get-tuple-element.699, bf16[4,64,3072]{2,1,0:T(8,128)(2,1)} %all-gather.2.cloned.1.call-done, ...), kind=kOutput, calls=%fused_computation.17.clone.1 | convolution fusion | flops 3225943808 | bytes 18351108 | tf_op jit(solution)/shard_map/while/body/eval_jaxpr/scw,fw->scf/dot_general | solution.py:39
  347.7 10.7 %fusion.129 = f32[4,64,3072]{2,1,0:T(8,128)} fusion(bf16[3072,2048]{1,0:T(8,128)(2,1)} %get-tuple-element.701, f32[4,64,2048]{2,1,0:T(8,128)S(1)} %get-tuple-element.640, bf16[1,2,4,64,2048]{4,3,2,1,0:T(8,128)(2,1)S(1)} %copy-done.6, s32[]{:T(128)S(6)} %min.13), kind=kOutput, calls=%fused_computation.2.clone.1 | convolution fusion | flops 3224895488 | bytes 18874372 | tf_op jit(solution)/shard_map/while/body/eval_jaxpr/scf,df->scd/dot_general | solution.py:80
  358.4 11.6 %fusion.130 = f32[4,64,3072]{2,1,0:T(8,128)} fusion(f32[4,64,3072]{2,1,0:T(8,128)} %fusion.129, bf16[3072,2048]{1,0:T(8,128)(2,1)} %get-tuple-element.700, f32[4,64,2048]{2,1,0:T(8,128)} %copy-done.7, bf16[1,2,4,64,2048]{4,3,2,1,0:T(8,128)(2,1)S(1)} %copy-done.6, s32[]{:T(128)S(6)} %min.13, bf16[1,2,4,64,2048]{4,3,2,1,0:T(8,128)(2,1)S(1)} %copy-done.5), kind=kOutput, calls=%fused_computation.8.clone.1 | convolution fusion | flops 3228303360 | bytes 23068676 | tf_op jit(solution)/shard_map/while/body/eval_jaxpr/scf,df->scd/dot_general | solution.py:79
  371.1 5.9 %psum.62 = f32[80]{0:T(128)S(1)} all-reduce(f32[80]{0:T(128)S(1)} %fusion.125), channel_id=1, replica_groups=mesh['section'=2,'expert'=4,'tensor'=4] {'tensor'}, use_global_device_ids=true, to_apply=%region_2.2 | all-reduce | flops 80 | bytes 640 | tf_op jit(solution)/shard_map/while/body/eval_jaxpr/psum | solution.py:43
  387.5 20.5 %reduce-scatter.2.cloned.1.call-done = f32[4,64,768]{2,1,0:T(8,128)} async-done(((f32[4,64,3072]{2,1,0:T(8,128)}), f32[4,64,768]{2,1,0:T(8,128)}) %reduce-scatter.2.cloned.1.call-update) | async-done | bytes 786448 | tf_op jit(solution)/shard_map/while/body/eval_jaxpr/reduce_scatter | solution.py:82
  414.1 6.0 %all-reduce.3 = (f32[80,2]{0,1:T(2,128)S(1)}, f32[80,4]{0,1:T(4,128)S(1)}) all-reduce(f32[80,2]{0,1:T(2,128)S(1)} %bitcast.172, f32[80,4]{0,1:T(4,128)S(1)} %fusion.126), channel_id=1, replica_groups=mesh['section'=2,'expert'=4,'tensor'=4] {'tensor'}, use_global_device_ids=true, to_apply=%region_11.11 | all-reduce | flops 480 | bytes 3840 | tf_op jit(solution)/shard_map/while/body/eval_jaxpr/psum | solution.py:97
  420.5 12.0 %all-to-all-done.2 = f32[4,64,768]{2,1,0:T(8,128)S(1)} async-done(((f32[4,64,768]{2,1,0:T(8,128)}), f32[4,64,768]{2,1,0:T(8,128)S(1)}, u32[]{:S(2)}, u32[]{:S(2)}) %all-to-all-start.2) | async-done | bytes 786464 | tf_op jit(solution)/shard_map/while/body/eval_jaxpr/all_to_all | solution.py:84
  433.2 5.9 %psum.63 = f32[80]{0:T(128)S(1)} all-reduce(f32[80]{0:T(128)S(1)} %get-tuple-element.643), channel_id=1, replica_groups=mesh['section'=2,'expert'=4,'tensor'=4] {'tensor'}, use_global_device_ids=true, to_apply=%region_13.13 | all-reduce | flops 80 | bytes 640 | tf_op jit(solution)/shard_map/while/body/eval_jaxpr/psum | solution.py:104
  (184 shorter events, 88.1 us)
Async XLA Ops:
  7.3 41.9 %copy-start.5 = (bf16[1,2,4,64,2048]{4,3,2,1,0:T(8,128)(2,1)S(1)}, bf16[1,2,4,64,2048]{4,3,2,1,0:T(8,128)(2,1)}, u32[]{:S(2)}) copy-start(bf16[1,2,4,64,2048]{4,3,2,1,0:T(8,128)(2,1)} %get-tuple-element.698) | copy-start | bytes 6291460 | tf_op jit(solution)/shard_map/while
  7.3 41.9 %all-gather.2.cloned.1.call-start = ((), (), s32[]{:S(2)}) async-start(), calls=%async_computation.4 | async-start | bytes 1966080 | tf_op jit(solution)/shard_map/while/body/eval_jaxpr/all_gather | solution.py:70
  30.3 89.0 %reduce-scatter.2.cloned.1.call-start = ((), (), s32[]{:S(2)}) async-start(), calls=%async_computation.5 | async-start | bytes 3932160 | tf_op jit(solution)/shard_map/while/body/eval_jaxpr/reduce_scatter | solution.py:82
  49.2 9.9 %copy-start.6 = (bf16[1,2,4,64,2048]{4,3,2,1,0:T(8,128)(2,1)S(1)}, bf16[1,2,4,64,2048]{4,3,2,1,0:T(8,128)(2,1)}, u32[]{:S(2)}) copy-start(bf16[1,2,4,64,2048]{4,3,2,1,0:T(8,128)(2,1)} %get-tuple-element.699) | copy-start | bytes 6291460 | tf_op jit(solution)/shard_map/while
  59.1 10.7 %copy-start.7 = (f32[4,64,2048]{2,1,0:T(8,128)}, f32[4,64,2048]{2,1,0:T(8,128)S(1)}, u32[]{:S(2)}) copy-start(f32[4,64,2048]{2,1,0:T(8,128)S(1)} %get-tuple-element.640) | copy-start | bytes 6291460 | tf_op jit(solution)/shard_map/while
  81.4 7.0 %copy-start.3 = (bf16[768,4]{0,1:T(4,128)(2,1)S(1)}, bf16[768,4]{0,1:T(4,128)(2,1)}, u32[]{:S(2)}) copy-start(bf16[768,4]{0,1:T(4,128)(2,1)} %get-tuple-element.696) | copy-start | bytes 18436 | tf_op jit(solution)/shard_map/while
  81.4 11.9 %copy-start.4 = (s32[1,2,80,2]{2,3,1,0:T(2,128)S(1)}, s32[1,2,80,2]{2,3,1,0:T(2,128)}, u32[]{:S(2)}) copy-start(s32[1,2,80,2]{2,3,1,0:T(2,128)} %get-tuple-element.694) | copy-start | bytes 3844 | tf_op jit(solution)/shard_map/while
  81.4 69.1 %copy-start.1 = (bf16[2,80,768]{2,1,0:T(8,128)(2,1)S(1)}, bf16[2,80,768]{2,1,0:T(8,128)(2,1)}, u32[]{:S(2)}) copy-start(bf16[2,80,768]{2,1,0:T(8,128)(2,1)} %get-tuple-element.692) | copy-start | bytes 737284 | tf_op jit(solution)/shard_map/while
  88.6 10.3 %all-to-all-start.1 = ((f32[4,1,64]{2,1,0:T(1,128)}), f32[4,1,64]{2,1,0:T(1,128)S(1)}, u32[]{:S(2)}, u32[]{:S(2)}) async-start(f32[4,1,64]{2,1,0:T(1,128)} %bitcast.160), calls=%async_computation.1 | async-start | bytes 4096 | tf_op jit(solution)/shard_map/while/body/eval_jaxpr/all_to_all | solution.py:85
  119.3 24.5 %all-to-all-start.2 = ((f32[4,64,768]{2,1,0:T(8,128)}), f32[4,64,768]{2,1,0:T(8,128)S(1)}, u32[]{:S(2)}, u32[]{:S(2)}) async-start(f32[4,64,768]{2,1,0:T(8,128)} %reduce-scatter.2.cloned.1.call-done), calls=%async_computation.3 | async-start | bytes 1572864 | tf_op jit(solution)/shard_map/while/body/eval_jaxpr/all_to_all | solution.py:84
  150.7 6.8 %collective-permute-start = (bf16[80,768]{1,0:T(8,128)(2,1)S(1)}, bf16[80,768]{1,0:T(8,128)(2,1)S(1)}, u32[]{:S(2)}, u32[]{:S(2)}) collective-permute-start(bf16[80,768]{1,0:T(8,128)(2,1)S(1)} %get-tuple-element.645), channel_id=1, source_target_pairs={{16,0},{17,1},{18,2},{19,3},{20,4},{21,5},{22,6},{23,7},{24,8},{25... | collective-permute-start | bytes 368648 | tf_op jit(solution)/shard_map/while/body/eval_jaxpr/ppermute | solution.py:13
  157.5 36.0 %copy-start.5 = (bf16[1,2,4,64,2048]{4,3,2,1,0:T(8,128)(2,1)S(1)}, bf16[1,2,4,64,2048]{4,3,2,1,0:T(8,128)(2,1)}, u32[]{:S(2)}) copy-start(bf16[1,2,4,64,2048]{4,3,2,1,0:T(8,128)(2,1)} %get-tuple-element.698) | copy-start | bytes 6291460 | tf_op jit(solution)/shard_map/while
  157.5 36.0 %all-gather.2.cloned.1.call-start = ((), (), s32[]{:S(2)}) async-start(), calls=%async_computation.4 | async-start | bytes 1966080 | tf_op jit(solution)/shard_map/while/body/eval_jaxpr/all_gather | solution.py:70
  176.1 87.5 %reduce-scatter.2.cloned.1.call-start = ((), (), s32[]{:S(2)}) async-start(), calls=%async_computation.5 | async-start | bytes 3932160 | tf_op jit(solution)/shard_map/while/body/eval_jaxpr/reduce_scatter | solution.py:82
  193.5 9.9 %copy-start.6 = (bf16[1,2,4,64,2048]{4,3,2,1,0:T(8,128)(2,1)S(1)}, bf16[1,2,4,64,2048]{4,3,2,1,0:T(8,128)(2,1)}, u32[]{:S(2)}) copy-start(bf16[1,2,4,64,2048]{4,3,2,1,0:T(8,128)(2,1)} %get-tuple-element.699) | copy-start | bytes 6291460 | tf_op jit(solution)/shard_map/while
  203.3 10.7 %copy-start.7 = (f32[4,64,2048]{2,1,0:T(8,128)}, f32[4,64,2048]{2,1,0:T(8,128)S(1)}, u32[]{:S(2)}) copy-start(f32[4,64,2048]{2,1,0:T(8,128)S(1)} %get-tuple-element.640) | copy-start | bytes 6291460 | tf_op jit(solution)/shard_map/while
  225.7 11.9 %copy-start.4 = (s32[1,2,80,2]{2,3,1,0:T(2,128)S(1)}, s32[1,2,80,2]{2,3,1,0:T(2,128)}, u32[]{:S(2)}) copy-start(s32[1,2,80,2]{2,3,1,0:T(2,128)} %get-tuple-element.694) | copy-start | bytes 3844 | tf_op jit(solution)/shard_map/while
  225.7 69.1 %copy-start.1 = (bf16[2,80,768]{2,1,0:T(8,128)(2,1)S(1)}, bf16[2,80,768]{2,1,0:T(8,128)(2,1)}, u32[]{:S(2)}) copy-start(bf16[2,80,768]{2,1,0:T(8,128)(2,1)} %get-tuple-element.692) | copy-start | bytes 737284 | tf_op jit(solution)/shard_map/while
  232.8 10.3 %all-to-all-start.1 = ((f32[4,1,64]{2,1,0:T(1,128)}), f32[4,1,64]{2,1,0:T(1,128)S(1)}, u32[]{:S(2)}, u32[]{:S(2)}) async-start(f32[4,1,64]{2,1,0:T(1,128)} %bitcast.160), calls=%async_computation.1 | async-start | bytes 4096 | tf_op jit(solution)/shard_map/while/body/eval_jaxpr/all_to_all | solution.py:85
  263.6 24.5 %all-to-all-start.2 = ((f32[4,64,768]{2,1,0:T(8,128)}), f32[4,64,768]{2,1,0:T(8,128)S(1)}, u32[]{:S(2)}, u32[]{:S(2)}) async-start(f32[4,64,768]{2,1,0:T(8,128)} %reduce-scatter.2.cloned.1.call-done), calls=%async_computation.3 | async-start | bytes 1572864 | tf_op jit(solution)/shard_map/while/body/eval_jaxpr/all_to_all | solution.py:84
  295.0 6.8 %collective-permute-start = (bf16[80,768]{1,0:T(8,128)(2,1)S(1)}, bf16[80,768]{1,0:T(8,128)(2,1)S(1)}, u32[]{:S(2)}, u32[]{:S(2)}) collective-permute-start(bf16[80,768]{1,0:T(8,128)(2,1)S(1)} %get-tuple-element.645), channel_id=1, source_target_pairs={{16,0},{17,1},{18,2},{19,3},{20,4},{21,5},{22,6},{23,7},{24,8},{25... | collective-permute-start | bytes 368648 | tf_op jit(solution)/shard_map/while/body/eval_jaxpr/ppermute | solution.py:13
  301.8 36.0 %copy-start.5 = (bf16[1,2,4,64,2048]{4,3,2,1,0:T(8,128)(2,1)S(1)}, bf16[1,2,4,64,2048]{4,3,2,1,0:T(8,128)(2,1)}, u32[]{:S(2)}) copy-start(bf16[1,2,4,64,2048]{4,3,2,1,0:T(8,128)(2,1)} %get-tuple-element.698) | copy-start | bytes 6291460 | tf_op jit(solution)/shard_map/while
  301.8 36.0 %all-gather.2.cloned.1.call-start = ((), (), s32[]{:S(2)}) async-start(), calls=%async_computation.4 | async-start | bytes 1966080 | tf_op jit(solution)/shard_map/while/body/eval_jaxpr/all_gather | solution.py:70
  320.4 87.5 %reduce-scatter.2.cloned.1.call-start = ((), (), s32[]{:S(2)}) async-start(), calls=%async_computation.5 | async-start | bytes 3932160 | tf_op jit(solution)/shard_map/while/body/eval_jaxpr/reduce_scatter | solution.py:82
  337.8 9.9 %copy-start.6 = (bf16[1,2,4,64,2048]{4,3,2,1,0:T(8,128)(2,1)S(1)}, bf16[1,2,4,64,2048]{4,3,2,1,0:T(8,128)(2,1)}, u32[]{:S(2)}) copy-start(bf16[1,2,4,64,2048]{4,3,2,1,0:T(8,128)(2,1)} %get-tuple-element.699) | copy-start | bytes 6291460 | tf_op jit(solution)/shard_map/while
  347.7 10.7 %copy-start.7 = (f32[4,64,2048]{2,1,0:T(8,128)}, f32[4,64,2048]{2,1,0:T(8,128)S(1)}, u32[]{:S(2)}) copy-start(f32[4,64,2048]{2,1,0:T(8,128)S(1)} %get-tuple-element.640) | copy-start | bytes 6291460 | tf_op jit(solution)/shard_map/while
  370.0 7.0 %copy-start.3 = (bf16[768,4]{0,1:T(4,128)(2,1)S(1)}, bf16[768,4]{0,1:T(4,128)(2,1)}, u32[]{:S(2)}) copy-start(bf16[768,4]{0,1:T(4,128)(2,1)} %get-tuple-element.696) | copy-start | bytes 18436 | tf_op jit(solution)/shard_map/while
  370.0 11.9 %copy-start.4 = (s32[1,2,80,2]{2,3,1,0:T(2,128)S(1)}, s32[1,2,80,2]{2,3,1,0:T(2,128)}, u32[]{:S(2)}) copy-start(s32[1,2,80,2]{2,3,1,0:T(2,128)} %get-tuple-element.694) | copy-start | bytes 3844 | tf_op jit(solution)/shard_map/while
  370.0 69.1 %copy-start.1 = (bf16[2,80,768]{2,1,0:T(8,128)(2,1)S(1)}, bf16[2,80,768]{2,1,0:T(8,128)(2,1)}, u32[]{:S(2)}) copy-start(bf16[2,80,768]{2,1,0:T(8,128)(2,1)} %get-tuple-element.692) | copy-start | bytes 737284 | tf_op jit(solution)/shard_map/while
  377.2 10.3 %all-to-all-start.1 = ((f32[4,1,64]{2,1,0:T(1,128)}), f32[4,1,64]{2,1,0:T(1,128)S(1)}, u32[]{:S(2)}, u32[]{:S(2)}) async-start(f32[4,1,64]{2,1,0:T(1,128)} %bitcast.160), calls=%async_computation.1 | async-start | bytes 4096 | tf_op jit(solution)/shard_map/while/body/eval_jaxpr/all_to_all | solution.py:85
  407.9 24.5 %all-to-all-start.2 = ((f32[4,64,768]{2,1,0:T(8,128)}), f32[4,64,768]{2,1,0:T(8,128)S(1)}, u32[]{:S(2)}, u32[]{:S(2)}) async-start(f32[4,64,768]{2,1,0:T(8,128)} %reduce-scatter.2.cloned.1.call-done), calls=%async_computation.3 | async-start | bytes 1572864 | tf_op jit(solution)/shard_map/while/body/eval_jaxpr/all_to_all | solution.py:84
  439.3 6.8 %collective-permute-start = (bf16[80,768]{1,0:T(8,128)(2,1)S(1)}, bf16[80,768]{1,0:T(8,128)(2,1)S(1)}, u32[]{:S(2)}, u32[]{:S(2)}) collective-permute-start(bf16[80,768]{1,0:T(8,128)(2,1)S(1)} %get-tuple-element.645), channel_id=1, source_target_pairs={{16,0},{17,1},{18,2},{19,3},{20,4},{21,5},{22,6},{23,7},{24,8},{25... | collective-permute-start | bytes 368648 | tf_op jit(solution)/shard_map/while/body/eval_jaxpr/ppermute | solution.py:13
  (5 other events, 10.5 us)
Sparse Core Ops, SparseCore 0:
  30.4 18.7 all-gather.1
  81.6 37.7 reduce-scatter.1
  176.2 17.1 all-gather.1
  225.8 37.7 reduce-scatter.1
  320.5 17.2 all-gather.1
  370.2 37.7 reduce-scatter.1
where the time goes:
time: 455 us; the launch traced here: 454 us
  waiting for transfers between devices  184 us (40%)
  matrix products  105 us (23%)
  blocking collectives  98.8 us (22%)
  starting transfers between devices  32.2 us (7%)
  between operations  13.4 us (3%)
  other arithmetic  10.5 us (2%)
  local copies, waits for them, and re-layouts  10 us (2%)
    reduce_scatter x3, waiting for transfers between devices, layer_back(): lax.psum_scatter(unit, 'tensor', scatter_dimension=2, tiled=True)  61.5 us
    all_gather x3, waiting for transfers between devices, layer_back(): lax.all_gather(arrived, 'tensor', axis=2, tiled=True)  53.5 us
    all_to_all x3, blocking collectives, layer_back(): lax.all_to_all(copies, 'expert', split_axis=0, concat_axis=0, tiled=True)  45.2 us
    all_to_all x3, waiting for transfers between devices, layer_back(): lax.all_to_all(unit_share, 'expert', split_axis=0, concat_axis=0, tiled=T...  35.9 us
    dot_general x3, matrix products, layer_back(): jnp.einsum('scf,df->scd', gate_grad, gate_mat, preferred_element_type=jnp...  34.9 us
    dot_general x3, matrix products, layer_back(): jnp.einsum('scf,df->scd', up_grad, up_mat, preferred_element_type=jnp.flo...  32.1 us
    dot_general x3, matrix products, add_columns(): jnp.einsum('scw,fw->scf', piece, down_mat, preferred_element_type=jnp.flo...  29.6 us
    psum x3, blocking collectives, layer_back(): prob_grad = lax.psum(prob_part, 'tensor')  18.1 us
  transfers between devices with their start and end apart: 15, of which 15 were waited for; matrix products, arithmetic and copies ran while one was open for 1% of the time, Pallas kernels for 0%

commit v1 on v0

--- a/solution.py
+++ b/solution.py
@@ -67,7 +67,7 @@
             (experts, group, capacity, quarter),
         ).reshape(holders, capacity, quarter)
         arrived = lax.all_to_all(copies, "expert", split_axis=0, concat_axis=0, tiled=True)
-        back_act = add_columns(lax.all_gather(arrived, "tensor", axis=2, tiled=True))
+        back_act = add_columns(jnp.concatenate(lax.all_gather(arrived, "tensor"), axis=2))
         gate_act = gate_saved.astype(jnp.float32)
         up_act = up_saved.astype(jnp.float32)
         sigma = jax.nn.sigmoid(gate_act)

time: 455 us -> 465 us (1.022)
  local copies, waits for them, and re-layouts: 10 us -> 21 us
    all_gather x0 -> x3, local copies, waits for them, and re-layouts: none -> 7.87 us  [layer_back(): lax.all_gather(arrived, 'tensor')]
where the time goes in v1:
time: 465 us; the launch traced here: 464 us
  waiting for transfers between devices  184 us (40%)
  matrix products  104 us (22%)
  blocking collectives  98.8 us (21%)
  starting transfers between devices  32.2 us (7%)
  local copies, waits for them, and re-layouts  21 us (5%)
  between operations  13.4 us (3%)
  other arithmetic  10.5 us (2%)
    reduce_scatter x3, waiting for transfers between devices, layer_back(): lax.psum_scatter(unit, 'tensor', scatter_dimension=2, tiled=True)  61.5 us
    all_gather x3, waiting for transfers between devices, layer_back(): lax.all_gather(arrived, 'tensor')  53.4 us
    all_to_all x3, blocking collectives, layer_back(): lax.all_to_all(copies, 'expert', split_axis=0, concat_axis=0, tiled=True)  45.2 us
    all_to_all x3, waiting for transfers between devices, layer_back(): lax.all_to_all(unit_share, 'expert', split_axis=0, concat_axis=0, tiled=T...  35.9 us
    dot_general x3, matrix products, layer_back(): jnp.einsum('scf,df->scd', gate_grad, gate_mat, preferred_element_type=jnp...  34.9 us
    dot_general x3, matrix products, layer_back(): jnp.einsum('scf,df->scd', up_grad, up_mat, preferred_element_type=jnp.flo...  32.2 us
    dot_general x3, matrix products, add_columns(): jnp.einsum('scw,fw->scf', piece, down_mat, preferred_element_type=jnp.flo...  29.1 us
    psum x3, blocking collectives, layer_back(): prob_grad = lax.psum(prob_part, 'tensor')  18.1 us
  transfers between devices with their start and end apart: 15, of which 15 were waited for; matrix products, arithmetic and copies ran while one was open for 1% of the time, Pallas kernels for 0%

profile of v1, /device:TPU:0, one launch (start us, length us, event | category | flops | bytes accessed | tf_op | source)
XLA Modules:
  0.0 464.3 jit_solution(16338299104533568551)
XLA Ops:
  7.3 449.4 %while.19 = (s32[]{:T(128)}, bf16[80,768]{1,0:T(8,128)(2,1)S(1)}, bf16[2,80,768]{2,1,0:T(8,128)(2,1)S(1)}, s32[]{:T(128)}, pred[]{:T(512)}, /*index=5*/bf16[2,80...) while((s32[]{:T(128)}, bf16[80,768]{1,0:T(8,128)(2,1)S(1)}, ...), condition=%wide.region_14.15_spmd.clone.clone, body=%wide.region_0.14_spmd.clone.clone.sunk | while | flops 9905498112 | bytes 127502008 | solution.py:132
  12.2 17.9 %all_to_all.47 = bf16[4,64,768]{2,1,0:T(8,128)(2,1)} all-to-all(bf16[4,64,768]{2,1,0:T(8,128)(2,1)S(1)} %bitcast.176), channel_id=1, replica_groups=mesh['section'=2,'expert'=4,'tensor'=4] {'expert'}, dimensions={0} | all-to-all | bytes 786432 | tf_op jit(solution)/shard_map/while/body/eval_jaxpr/all_to_all | solution.py:69
  30.2 18.9 %all-gather.6.cloned.1.call-done = bf16[16,64,768]{2,1,0:T(8,128)(2,1)} async-done(((bf16[4,64,768]{2,1,0:T(8,128)(2,1)}), bf16[16,64,768]{2,1,0:T(8,128)(2,1)}) %all-gather.6.cloned.1.call-update) | async-done | bytes 1572880 | tf_op jit(solution)/shard_map/while/body/eval_jaxpr/all_gather | solution.py:70
  52.9 9.7 %fusion.123 = (f32[4,64]{1,0:T(4,128)}, f32[4,64,2048]{2,1,0:T(8,128)S(1)}) fusion(bf16[1,2,4,64,2048]{4,3,2,1,0:T(8,128)(2,1)} %get-tuple-element.698, s32[]{:T(128)S(6)} %min.13, bf16[1,2,4,64,2048]{4,3,2,1,0:T(8,128)(2,1)} %get-tuple-element.699, bf16[4,64,3072]{2,1,0:T(8,128)(2,1)S(1)} %reshape.314, bf16[2048,3072]{1,0:T(8,128)(2,1)} %get-tuple-element.697), kind=kOutput, calls=%fused_computation.17.clone.1 | convolution fusion | flops 3225943808 | bytes 18351108 | tf_op jit(solution)/shard_map/while/body/eval_jaxpr/scw,fw->scf/dot_general | solution.py:39
  62.6 10.7 %fusion.129 = f32[4,64,3072]{2,1,0:T(8,128)} fusion(bf16[3072,2048]{1,0:T(8,128)(2,1)} %get-tuple-element.701, f32[4,64,2048]{2,1,0:T(8,128)S(1)} %get-tuple-element.640, bf16[1,2,4,64,2048]{4,3,2,1,0:T(8,128)(2,1)S(1)} %copy-done.6, s32[]{:T(128)S(6)} %min.13), kind=kOutput, calls=%fused_computation.2.clone.1 | convolution fusion | flops 3224895488 | bytes 18874372 | tf_op jit(solution)/shard_map/while/body/eval_jaxpr/scf,df->scd/dot_general | solution.py:80
  73.3 11.6 %fusion.130 = f32[4,64,3072]{2,1,0:T(8,128)} fusion(f32[4,64,3072]{2,1,0:T(8,128)} %fusion.129, bf16[3072,2048]{1,0:T(8,128)(2,1)} %get-tuple-element.700, f32[4,64,2048]{2,1,0:T(8,128)} %copy-done.8, bf16[1,2,4,64,2048]{4,3,2,1,0:T(8,128)(2,1)S(1)} %copy-done.7, s32[]{:T(128)S(6)} %min.13, bf16[1,2,4,64,2048]{4,3,2,1,0:T(8,128)(2,1)S(1)} %copy-done.5), kind=kOutput, calls=%fused_computation.8.clone.1 | convolution fusion | flops 3228303360 | bytes 23068676 | tf_op jit(solution)/shard_map/while/body/eval_jaxpr/scf,df->scd/dot_general | solution.py:79
  86.0 5.9 %psum.62 = f32[80]{0:T(128)S(1)} all-reduce(f32[80]{0:T(128)S(1)} %fusion.125), channel_id=1, replica_groups=mesh['section'=2,'expert'=4,'tensor'=4] {'tensor'}, use_global_device_ids=true, to_apply=%region_2.2 | all-reduce | flops 80 | bytes 640 | tf_op jit(solution)/shard_map/while/body/eval_jaxpr/psum | solution.py:43
  96.9 5.5 %all-to-all-done.1 = f32[4,1,64]{2,1,0:T(1,128)S(1)} async-done(((f32[4,1,64]{2,1,0:T(1,128)}), f32[4,1,64]{2,1,0:T(1,128)S(1)}, u32[]{:S(2)}, u32[]{:S(2)}) %all-to-all-start.1) | async-done | bytes 1056 | tf_op jit(solution)/shard_map/while/body/eval_jaxpr/all_to_all | solution.py:85
  102.4 20.5 %reduce-scatter.2.cloned.1.call-done = f32[4,64,768]{2,1,0:T(8,128)} async-done(((f32[4,64,3072]{2,1,0:T(8,128)}), f32[4,64,768]{2,1,0:T(8,128)}) %reduce-scatter.2.cloned.1.call-update) | async-done | bytes 786448 | tf_op jit(solution)/shard_map/while/body/eval_jaxpr/reduce_scatter | solution.py:82
  129.1 6.0 %all-reduce.3 = (f32[80,2]{0,1:T(2,128)S(1)}, f32[80,4]{0,1:T(4,128)S(1)}) all-reduce(f32[80,2]{0,1:T(2,128)S(1)} %bitcast.182, f32[80,4]{0,1:T(4,128)S(1)} %fusion.126), channel_id=1, replica_groups=mesh['section'=2,'expert'=4,'tensor'=4] {'tensor'}, use_global_device_ids=true, to_apply=%region_11.11 | all-reduce | flops 480 | bytes 3840 | tf_op jit(solution)/shard_map/while/body/eval_jaxpr/psum | solution.py:97
  135.5 12.0 %all-to-all-done.2 = f32[4,64,768]{2,1,0:T(8,128)S(1)} async-done(((f32[4,64,768]{2,1,0:T(8,128)}), f32[4,64,768]{2,1,0:T(8,128)S(1)}, u32[]{:S(2)}, u32[]{:S(2)}) %all-to-all-start.2) | async-done | bytes 786464 | tf_op jit(solution)/shard_map/while/body/eval_jaxpr/all_to_all | solution.py:84
  148.2 5.9 %psum.63 = f32[80]{0:T(128)S(1)} all-reduce(f32[80]{0:T(128)S(1)} %get-tuple-element.643), channel_id=1, replica_groups=mesh['section'=2,'expert'=4,'tensor'=4] {'tensor'}, use_global_device_ids=true, to_apply=%region_13.13 | all-reduce | flops 80 | bytes 640 | tf_op jit(solution)/shard_map/while/body/eval_jaxpr/psum | solution.py:104
  165.9 13.6 %all_to_all.47 = bf16[4,64,768]{2,1,0:T(8,128)(2,1)} all-to-all(bf16[4,64,768]{2,1,0:T(8,128)(2,1)S(1)} %bitcast.176), channel_id=1, replica_groups=mesh['section'=2,'expert'=4,'tensor'=4] {'expert'}, dimensions={0} | all-to-all | bytes 786432 | tf_op jit(solution)/shard_map/while/body/eval_jaxpr/all_to_all | solution.py:69
  179.6 17.3 %all-gather.6.cloned.1.call-done = bf16[16,64,768]{2,1,0:T(8,128)(2,1)} async-done(((bf16[4,64,768]{2,1,0:T(8,128)(2,1)}), bf16[16,64,768]{2,1,0:T(8,128)(2,1)}) %all-gather.6.cloned.1.call-update) | async-done | bytes 1572880 | tf_op jit(solution)/shard_map/while/body/eval_jaxpr/all_gather | solution.py:70
  200.7 9.7 %fusion.123 = (f32[4,64]{1,0:T(4,128)}, f32[4,64,2048]{2,1,0:T(8,128)S(1)}) fusion(bf16[1,2,4,64,2048]{4,3,2,1,0:T(8,128)(2,1)} %get-tuple-element.698, s32[]{:T(128)S(6)} %min.13, bf16[1,2,4,64,2048]{4,3,2,1,0:T(8,128)(2,1)} %get-tuple-element.699, bf16[4,64,3072]{2,1,0:T(8,128)(2,1)S(1)} %reshape.314, bf16[2048,3072]{1,0:T(8,128)(2,1)} %get-tuple-element.697), kind=kOutput, calls=%fused_computation.17.clone.1 | convolution fusion | flops 3225943808 | bytes 18351108 | tf_op jit(solution)/shard_map/while/body/eval_jaxpr/scw,fw->scf/dot_general | solution.py:39
  210.4 10.7 %fusion.129 = f32[4,64,3072]{2,1,0:T(8,128)} fusion(bf16[3072,2048]{1,0:T(8,128)(2,1)} %get-tuple-element.701, f32[4,64,2048]{2,1,0:T(8,128)S(1)} %get-tuple-element.640, bf16[1,2,4,64,2048]{4,3,2,1,0:T(8,128)(2,1)S(1)} %copy-done.6, s32[]{:T(128)S(6)} %min.13), kind=kOutput, calls=%fused_computation.2.clone.1 | convolution fusion | flops 3224895488 | bytes 18874372 | tf_op jit(solution)/shard_map/while/body/eval_jaxpr/scf,df->scd/dot_general | solution.py:80
  221.2 11.6 %fusion.130 = f32[4,64,3072]{2,1,0:T(8,128)} fusion(f32[4,64,3072]{2,1,0:T(8,128)} %fusion.129, bf16[3072,2048]{1,0:T(8,128)(2,1)} %get-tuple-element.700, f32[4,64,2048]{2,1,0:T(8,128)} %copy-done.8, bf16[1,2,4,64,2048]{4,3,2,1,0:T(8,128)(2,1)S(1)} %copy-done.7, s32[]{:T(128)S(6)} %min.13, bf16[1,2,4,64,2048]{4,3,2,1,0:T(8,128)(2,1)S(1)} %copy-done.5), kind=kOutput, calls=%fused_computation.8.clone.1 | convolution fusion | flops 3228303360 | bytes 23068676 | tf_op jit(solution)/shard_map/while/body/eval_jaxpr/scf,df->scd/dot_general | solution.py:79
  233.9 5.9 %psum.62 = f32[80]{0:T(128)S(1)} all-reduce(f32[80]{0:T(128)S(1)} %fusion.125), channel_id=1, replica_groups=mesh['section'=2,'expert'=4,'tensor'=4] {'tensor'}, use_global_device_ids=true, to_apply=%region_2.2 | all-reduce | flops 80 | bytes 640 | tf_op jit(solution)/shard_map/while/body/eval_jaxpr/psum | solution.py:43
  250.2 20.5 %reduce-scatter.2.cloned.1.call-done = f32[4,64,768]{2,1,0:T(8,128)} async-done(((f32[4,64,3072]{2,1,0:T(8,128)}), f32[4,64,768]{2,1,0:T(8,128)}) %reduce-scatter.2.cloned.1.call-update) | async-done | bytes 786448 | tf_op jit(solution)/shard_map/while/body/eval_jaxpr/reduce_scatter | solution.py:82
  276.9 6.1 %all-reduce.3 = (f32[80,2]{0,1:T(2,128)S(1)}, f32[80,4]{0,1:T(4,128)S(1)}) all-reduce(f32[80,2]{0,1:T(2,128)S(1)} %bitcast.182, f32[80,4]{0,1:T(4,128)S(1)} %fusion.126), channel_id=1, replica_groups=mesh['section'=2,'expert'=4,'tensor'=4] {'tensor'}, use_global_device_ids=true, to_apply=%region_11.11 | all-reduce | flops 480 | bytes 3840 | tf_op jit(solution)/shard_map/while/body/eval_jaxpr/psum | solution.py:97
  283.3 12.0 %all-to-all-done.2 = f32[4,64,768]{2,1,0:T(8,128)S(1)} async-done(((f32[4,64,768]{2,1,0:T(8,128)}), f32[4,64,768]{2,1,0:T(8,128)S(1)}, u32[]{:S(2)}, u32[]{:S(2)}) %all-to-all-start.2) | async-done | bytes 786464 | tf_op jit(solution)/shard_map/while/body/eval_jaxpr/all_to_all | solution.py:84
  296.0 5.9 %psum.63 = f32[80]{0:T(128)S(1)} all-reduce(f32[80]{0:T(128)S(1)} %get-tuple-element.643), channel_id=1, replica_groups=mesh['section'=2,'expert'=4,'tensor'=4] {'tensor'}, use_global_device_ids=true, to_apply=%region_13.13 | all-reduce | flops 80 | bytes 640 | tf_op jit(solution)/shard_map/while/body/eval_jaxpr/psum | solution.py:104
  313.7 13.6 %all_to_all.47 = bf16[4,64,768]{2,1,0:T(8,128)(2,1)} all-to-all(bf16[4,64,768]{2,1,0:T(8,128)(2,1)S(1)} %bitcast.176), channel_id=1, replica_groups=mesh['section'=2,'expert'=4,'tensor'=4] {'expert'}, dimensions={0} | all-to-all | bytes 786432 | tf_op jit(solution)/shard_map/while/body/eval_jaxpr/all_to_all | solution.py:69
  327.4 17.3 %all-gather.6.cloned.1.call-done = bf16[16,64,768]{2,1,0:T(8,128)(2,1)} async-done(((bf16[4,64,768]{2,1,0:T(8,128)(2,1)}), bf16[16,64,768]{2,1,0:T(8,128)(2,1)}) %all-gather.6.cloned.1.call-update) | async-done | bytes 1572880 | tf_op jit(solution)/shard_map/while/body/eval_jaxpr/all_gather | solution.py:70
  348.5 9.7 %fusion.123 = (f32[4,64]{1,0:T(4,128)}, f32[4,64,2048]{2,1,0:T(8,128)S(1)}) fusion(bf16[1,2,4,64,2048]{4,3,2,1,0:T(8,128)(2,1)} %get-tuple-element.698, s32[]{:T(128)S(6)} %min.13, bf16[1,2,4,64,2048]{4,3,2,1,0:T(8,128)(2,1)} %get-tuple-element.699, bf16[4,64,3072]{2,1,0:T(8,128)(2,1)S(1)} %reshape.314, bf16[2048,3072]{1,0:T(8,128)(2,1)} %get-tuple-element.697), kind=kOutput, calls=%fused_computation.17.clone.1 | convolution fusion | flops 3225943808 | bytes 18351108 | tf_op jit(solution)/shard_map/while/body/eval_jaxpr/scw,fw->scf/dot_general | solution.py:39
  358.3 10.7 %fusion.129 = f32[4,64,3072]{2,1,0:T(8,128)} fusion(bf16[3072,2048]{1,0:T(8,128)(2,1)} %get-tuple-element.701, f32[4,64,2048]{2,1,0:T(8,128)S(1)} %get-tuple-element.640, bf16[1,2,4,64,2048]{4,3,2,1,0:T(8,128)(2,1)S(1)} %copy-done.6, s32[]{:T(128)S(6)} %min.13), kind=kOutput, calls=%fused_computation.2.clone.1 | convolution fusion | flops 3224895488 | bytes 18874372 | tf_op jit(solution)/shard_map/while/body/eval_jaxpr/scf,df->scd/dot_general | solution.py:80
  369.0 11.6 %fusion.130 = f32[4,64,3072]{2,1,0:T(8,128)} fusion(f32[4,64,3072]{2,1,0:T(8,128)} %fusion.129, bf16[3072,2048]{1,0:T(8,128)(2,1)} %get-tuple-element.700, f32[4,64,2048]{2,1,0:T(8,128)} %copy-done.8, bf16[1,2,4,64,2048]{4,3,2,1,0:T(8,128)(2,1)S(1)} %copy-done.7, s32[]{:T(128)S(6)} %min.13, bf16[1,2,4,64,2048]{4,3,2,1,0:T(8,128)(2,1)S(1)} %copy-done.5), kind=kOutput, calls=%fused_computation.8.clone.1 | convolution fusion | flops 3228303360 | bytes 23068676 | tf_op jit(solution)/shard_map/while/body/eval_jaxpr/scf,df->scd/dot_general | solution.py:79
  381.7 5.9 %psum.62 = f32[80]{0:T(128)S(1)} all-reduce(f32[80]{0:T(128)S(1)} %fusion.125), channel_id=1, replica_groups=mesh['section'=2,'expert'=4,'tensor'=4] {'tensor'}, use_global_device_ids=true, to_apply=%region_2.2 | all-reduce | flops 80 | bytes 640 | tf_op jit(solution)/shard_map/while/body/eval_jaxpr/psum | solution.py:43
  398.1 20.5 %reduce-scatter.2.cloned.1.call-done = f32[4,64,768]{2,1,0:T(8,128)} async-done(((f32[4,64,3072]{2,1,0:T(8,128)}), f32[4,64,768]{2,1,0:T(8,128)}) %reduce-scatter.2.cloned.1.call-update) | async-done | bytes 786448 | tf_op jit(solution)/shard_map/while/body/eval_jaxpr/reduce_scatter | solution.py:82
  424.7 6.1 %all-reduce.3 = (f32[80,2]{0,1:T(2,128)S(1)}, f32[80,4]{0,1:T(4,128)S(1)}) all-reduce(f32[80,2]{0,1:T(2,128)S(1)} %bitcast.182, f32[80,4]{0,1:T(4,128)S(1)} %fusion.126), channel_id=1, replica_groups=mesh['section'=2,'expert'=4,'tensor'=4] {'tensor'}, use_global_device_ids=true, to_apply=%region_11.11 | all-reduce | flops 480 | bytes 3840 | tf_op jit(solution)/shard_map/while/body/eval_jaxpr/psum | solution.py:97
  431.2 12.0 %all-to-all-done.2 = f32[4,64,768]{2,1,0:T(8,128)S(1)} async-done(((f32[4,64,768]{2,1,0:T(8,128)}), f32[4,64,768]{2,1,0:T(8,128)S(1)}, u32[]{:S(2)}, u32[]{:S(2)}) %all-to-all-start.2) | async-done | bytes 786464 | tf_op jit(solution)/shard_map/while/body/eval_jaxpr/all_to_all | solution.py:84
  443.8 5.9 %psum.63 = f32[80]{0:T(128)S(1)} all-reduce(f32[80]{0:T(128)S(1)} %get-tuple-element.643), channel_id=1, replica_groups=mesh['section'=2,'expert'=4,'tensor'=4] {'tensor'}, use_global_device_ids=true, to_apply=%region_13.13 | all-reduce | flops 80 | bytes 640 | tf_op jit(solution)/shard_map/while/body/eval_jaxpr/psum | solution.py:104
  (196 shorter events, 99.1 us)
Async XLA Ops:
  7.3 41.7 %all-gather.6.cloned.1.call-start = ((), (), s32[]{:S(2)}) async-start(), calls=%async_computation.4 | async-start | bytes 1966080 | tf_op jit(solution)/shard_map/while/body/eval_jaxpr/all_gather | solution.py:70
  30.1 92.8 %reduce-scatter.2.cloned.1.call-start = ((), (), s32[]{:S(2)}) async-start(), calls=%async_computation.5 | async-start | bytes 3932160 | tf_op jit(solution)/shard_map/while/body/eval_jaxpr/reduce_scatter | solution.py:82
  52.9 9.7 %copy-start.6 = (bf16[1,2,4,64,2048]{4,3,2,1,0:T(8,128)(2,1)S(1)}, bf16[1,2,4,64,2048]{4,3,2,1,0:T(8,128)(2,1)}, u32[]{:S(2)}) copy-start(bf16[1,2,4,64,2048]{4,3,2,1,0:T(8,128)(2,1)} %get-tuple-element.699) | copy-start | bytes 6291460 | tf_op jit(solution)/shard_map/while
  62.6 10.7 %copy-start.8 = (f32[4,64,2048]{2,1,0:T(8,128)}, f32[4,64,2048]{2,1,0:T(8,128)S(1)}, u32[]{:S(2)}) copy-start(f32[4,64,2048]{2,1,0:T(8,128)S(1)} %get-tuple-element.640) | copy-start | bytes 6291460 | tf_op jit(solution)/shard_map/while
  62.6 10.7 %copy-start.5 = (bf16[1,2,4,64,2048]{4,3,2,1,0:T(8,128)(2,1)S(1)}, bf16[1,2,4,64,2048]{4,3,2,1,0:T(8,128)(2,1)}, u32[]{:S(2)}) copy-start(bf16[1,2,4,64,2048]{4,3,2,1,0:T(8,128)(2,1)} %get-tuple-element.698) | copy-start | bytes 6291460 | tf_op jit(solution)/shard_map/while
  62.6 10.7 %copy-start.7 = (bf16[1,2,4,64,2048]{4,3,2,1,0:T(8,128)(2,1)S(1)}, bf16[1,2,4,64,2048]{4,3,2,1,0:T(8,128)(2,1)}, u32[]{:S(2)}) copy-start(bf16[1,2,4,64,2048]{4,3,2,1,0:T(8,128)(2,1)} %get-tuple-element.699) | copy-start | bytes 6291460 | tf_op jit(solution)/shard_map/while
  85.0 11.9 %copy-start.4 = (s32[1,2,80,2]{2,3,1,0:T(2,128)S(1)}, s32[1,2,80,2]{2,3,1,0:T(2,128)}, u32[]{:S(2)}) copy-start(s32[1,2,80,2]{2,3,1,0:T(2,128)} %get-tuple-element.694) | copy-start | bytes 3844 | tf_op jit(solution)/shard_map/while
  85.0 69.1 %copy-start.1 = (bf16[2,80,768]{2,1,0:T(8,128)(2,1)S(1)}, bf16[2,80,768]{2,1,0:T(8,128)(2,1)}, u32[]{:S(2)}) copy-start(bf16[2,80,768]{2,1,0:T(8,128)(2,1)} %get-tuple-element.692) | copy-start | bytes 737284 | tf_op jit(solution)/shard_map/while
  92.1 10.3 %all-to-all-start.1 = ((f32[4,1,64]{2,1,0:T(1,128)}), f32[4,1,64]{2,1,0:T(1,128)S(1)}, u32[]{:S(2)}, u32[]{:S(2)}) async-start(f32[4,1,64]{2,1,0:T(1,128)} %bitcast.168), calls=%async_computation.1 | async-start | bytes 4096 | tf_op jit(solution)/shard_map/while/body/eval_jaxpr/all_to_all | solution.py:85
  122.9 24.5 %all-to-all-start.2 = ((f32[4,64,768]{2,1,0:T(8,128)}), f32[4,64,768]{2,1,0:T(8,128)S(1)}, u32[]{:S(2)}, u32[]{:S(2)}) async-start(f32[4,64,768]{2,1,0:T(8,128)} %reduce-scatter.2.cloned.1.call-done), calls=%async_computation.3 | async-start | bytes 1572864 | tf_op jit(solution)/shard_map/while/body/eval_jaxpr/all_to_all | solution.py:84
  154.3 6.8 %collective-permute-start = (bf16[80,768]{1,0:T(8,128)(2,1)S(1)}, bf16[80,768]{1,0:T(8,128)(2,1)S(1)}, u32[]{:S(2)}, u32[]{:S(2)}) collective-permute-start(bf16[80,768]{1,0:T(8,128)(2,1)S(1)} %get-tuple-element.645), channel_id=1, source_target_pairs={{16,0},{17,1},{18,2},{19,3},{20,4},{21,5},{22,6},{23,7},{24,8},{25... | collective-permute-start | bytes 368648 | tf_op jit(solution)/shard_map/while/body/eval_jaxpr/ppermute | solution.py:13
  161.0 35.8 %all-gather.6.cloned.1.call-start = ((), (), s32[]{:S(2)}) async-start(), calls=%async_computation.4 | async-start | bytes 1966080 | tf_op jit(solution)/shard_map/while/body/eval_jaxpr/all_gather | solution.py:70
  179.5 91.2 %reduce-scatter.2.cloned.1.call-start = ((), (), s32[]{:S(2)}) async-start(), calls=%async_computation.5 | async-start | bytes 3932160 | tf_op jit(solution)/shard_map/while/body/eval_jaxpr/reduce_scatter | solution.py:82
  200.7 9.7 %copy-start.6 = (bf16[1,2,4,64,2048]{4,3,2,1,0:T(8,128)(2,1)S(1)}, bf16[1,2,4,64,2048]{4,3,2,1,0:T(8,128)(2,1)}, u32[]{:S(2)}) copy-start(bf16[1,2,4,64,2048]{4,3,2,1,0:T(8,128)(2,1)} %get-tuple-element.699) | copy-start | bytes 6291460 | tf_op jit(solution)/shard_map/while
  210.4 10.7 %copy-start.8 = (f32[4,64,2048]{2,1,0:T(8,128)}, f32[4,64,2048]{2,1,0:T(8,128)S(1)}, u32[]{:S(2)}) copy-start(f32[4,64,2048]{2,1,0:T(8,128)S(1)} %get-tuple-element.640) | copy-start | bytes 6291460 | tf_op jit(solution)/shard_map/while
  210.4 10.7 %copy-start.5 = (bf16[1,2,4,64,2048]{4,3,2,1,0:T(8,128)(2,1)S(1)}, bf16[1,2,4,64,2048]{4,3,2,1,0:T(8,128)(2,1)}, u32[]{:S(2)}) copy-start(bf16[1,2,4,64,2048]{4,3,2,1,0:T(8,128)(2,1)} %get-tuple-element.698) | copy-start | bytes 6291460 | tf_op jit(solution)/shard_map/while
  210.4 10.7 %copy-start.7 = (bf16[1,2,4,64,2048]{4,3,2,1,0:T(8,128)(2,1)S(1)}, bf16[1,2,4,64,2048]{4,3,2,1,0:T(8,128)(2,1)}, u32[]{:S(2)}) copy-start(bf16[1,2,4,64,2048]{4,3,2,1,0:T(8,128)(2,1)} %get-tuple-element.699) | copy-start | bytes 6291460 | tf_op jit(solution)/shard_map/while
  232.8 11.9 %copy-start.4 = (s32[1,2,80,2]{2,3,1,0:T(2,128)S(1)}, s32[1,2,80,2]{2,3,1,0:T(2,128)}, u32[]{:S(2)}) copy-start(s32[1,2,80,2]{2,3,1,0:T(2,128)} %get-tuple-element.694) | copy-start | bytes 3844 | tf_op jit(solution)/shard_map/while
  232.8 69.1 %copy-start.1 = (bf16[2,80,768]{2,1,0:T(8,128)(2,1)S(1)}, bf16[2,80,768]{2,1,0:T(8,128)(2,1)}, u32[]{:S(2)}) copy-start(bf16[2,80,768]{2,1,0:T(8,128)(2,1)} %get-tuple-element.692) | copy-start | bytes 737284 | tf_op jit(solution)/shard_map/while
  240.0 10.3 %all-to-all-start.1 = ((f32[4,1,64]{2,1,0:T(1,128)}), f32[4,1,64]{2,1,0:T(1,128)S(1)}, u32[]{:S(2)}, u32[]{:S(2)}) async-start(f32[4,1,64]{2,1,0:T(1,128)} %bitcast.168), calls=%async_computation.1 | async-start | bytes 4096 | tf_op jit(solution)/shard_map/while/body/eval_jaxpr/all_to_all | solution.py:85
  270.7 24.5 %all-to-all-start.2 = ((f32[4,64,768]{2,1,0:T(8,128)}), f32[4,64,768]{2,1,0:T(8,128)S(1)}, u32[]{:S(2)}, u32[]{:S(2)}) async-start(f32[4,64,768]{2,1,0:T(8,128)} %reduce-scatter.2.cloned.1.call-done), calls=%async_computation.3 | async-start | bytes 1572864 | tf_op jit(solution)/shard_map/while/body/eval_jaxpr/all_to_all | solution.py:84
  302.1 6.8 %collective-permute-start = (bf16[80,768]{1,0:T(8,128)(2,1)S(1)}, bf16[80,768]{1,0:T(8,128)(2,1)S(1)}, u32[]{:S(2)}, u32[]{:S(2)}) collective-permute-start(bf16[80,768]{1,0:T(8,128)(2,1)S(1)} %get-tuple-element.645), channel_id=1, source_target_pairs={{16,0},{17,1},{18,2},{19,3},{20,4},{21,5},{22,6},{23,7},{24,8},{25... | collective-permute-start | bytes 368648 | tf_op jit(solution)/shard_map/while/body/eval_jaxpr/ppermute | solution.py:13
  308.9 35.8 %all-gather.6.cloned.1.call-start = ((), (), s32[]{:S(2)}) async-start(), calls=%async_computation.4 | async-start | bytes 1966080 | tf_op jit(solution)/shard_map/while/body/eval_jaxpr/all_gather | solution.py:70
  327.4 91.2 %reduce-scatter.2.cloned.1.call-start = ((), (), s32[]{:S(2)}) async-start(), calls=%async_computation.5 | async-start | bytes 3932160 | tf_op jit(solution)/shard_map/while/body/eval_jaxpr/reduce_scatter | solution.py:82
  358.3 10.7 %copy-start.8 = (f32[4,64,2048]{2,1,0:T(8,128)}, f32[4,64,2048]{2,1,0:T(8,128)S(1)}, u32[]{:S(2)}) copy-start(f32[4,64,2048]{2,1,0:T(8,128)S(1)} %get-tuple-element.640) | copy-start | bytes 6291460 | tf_op jit(solution)/shard_map/while
  358.3 10.7 %copy-start.5 = (bf16[1,2,4,64,2048]{4,3,2,1,0:T(8,128)(2,1)S(1)}, bf16[1,2,4,64,2048]{4,3,2,1,0:T(8,128)(2,1)}, u32[]{:S(2)}) copy-start(bf16[1,2,4,64,2048]{4,3,2,1,0:T(8,128)(2,1)} %get-tuple-element.698) | copy-start | bytes 6291460 | tf_op jit(solution)/shard_map/while
  358.3 10.7 %copy-start.7 = (bf16[1,2,4,64,2048]{4,3,2,1,0:T(8,128)(2,1)S(1)}, bf16[1,2,4,64,2048]{4,3,2,1,0:T(8,128)(2,1)}, u32[]{:S(2)}) copy-start(bf16[1,2,4,64,2048]{4,3,2,1,0:T(8,128)(2,1)} %get-tuple-element.699) | copy-start | bytes 6291460 | tf_op jit(solution)/shard_map/while
  380.6 11.9 %copy-start.4 = (s32[1,2,80,2]{2,3,1,0:T(2,128)S(1)}, s32[1,2,80,2]{2,3,1,0:T(2,128)}, u32[]{:S(2)}) copy-start(s32[1,2,80,2]{2,3,1,0:T(2,128)} %get-tuple-element.694) | copy-start | bytes 3844 | tf_op jit(solution)/shard_map/while
  380.7 69.1 %copy-start.1 = (bf16[2,80,768]{2,1,0:T(8,128)(2,1)S(1)}, bf16[2,80,768]{2,1,0:T(8,128)(2,1)}, u32[]{:S(2)}) copy-start(bf16[2,80,768]{2,1,0:T(8,128)(2,1)} %get-tuple-element.692) | copy-start | bytes 737284 | tf_op jit(solution)/shard_map/while
  387.8 10.3 %all-to-all-start.1 = ((f32[4,1,64]{2,1,0:T(1,128)}), f32[4,1,64]{2,1,0:T(1,128)S(1)}, u32[]{:S(2)}, u32[]{:S(2)}) async-start(f32[4,1,64]{2,1,0:T(1,128)} %bitcast.168), calls=%async_computation.1 | async-start | bytes 4096 | tf_op jit(solution)/shard_map/while/body/eval_jaxpr/all_to_all | solution.py:85
  418.6 24.5 %all-to-all-start.2 = ((f32[4,64,768]{2,1,0:T(8,128)}), f32[4,64,768]{2,1,0:T(8,128)S(1)}, u32[]{:S(2)}, u32[]{:S(2)}) async-start(f32[4,64,768]{2,1,0:T(8,128)} %reduce-scatter.2.cloned.1.call-done), calls=%async_computation.3 | async-start | bytes 1572864 | tf_op jit(solution)/shard_map/while/body/eval_jaxpr/all_to_all | solution.py:84
  450.0 6.8 %collective-permute-start = (bf16[80,768]{1,0:T(8,128)(2,1)S(1)}, bf16[80,768]{1,0:T(8,128)(2,1)S(1)}, u32[]{:S(2)}, u32[]{:S(2)}) collective-permute-start(bf16[80,768]{1,0:T(8,128)(2,1)S(1)} %get-tuple-element.645), channel_id=1, source_target_pairs={{16,0},{17,1},{18,2},{19,3},{20,4},{21,5},{22,6},{23,7},{24,8},{25... | collective-permute-start | bytes 368648 | tf_op jit(solution)/shard_map/while/body/eval_jaxpr/ppermute | solution.py:13
  (8 other events, 34.1 us)
Sparse Core Ops, SparseCore 0:
  30.3 18.7 all-gather.5
  85.1 37.7 reduce-scatter.1
  179.7 17.1 all-gather.5
  233.0 37.7 reduce-scatter.1
  327.5 17.1 all-gather.5
  380.8 37.7 reduce-scatter.1
